TPU v7x, 128 devices: a whole 4x4x4 slice. The times are simulated.
128 devices in a mesh: dp: 128 (over z, y, x, core).
Axes of the slice: x: 4, y: 4, z: 4, core: 2. Of those that a mesh axis runs over, the one named last changes fastest.
Arguments:
- grads: float32 [128, 4194304], P('dp')
- master: float32 [4194304], P('dp'), may hold values from -0.75 to 0.75
- m_old: float32 [128, 65536], P('dp'), may hold values from -6 to 6
- v_old: float32 [128, 65536], P('dp'), may hold values from 0.25 to 4
- old_bounds: int32 [129], replicated, may hold values from 0 to 4194304, as said below
Outputs:
- master_new: float32 [4194304], P('dp')
- m_new: float32 [4194304], P('dp')
- v_new: float32 [4194304], P('dp')
- params_full: bfloat16 [4194304], replicated
Inputs may be any that keep to these rules, and one draw needn't show every extreme that they name: old_bounds[0] = 0, the last entry is 4194304, entries never fall, and old_bounds[i] - i * 32768 lies between -16384 and 16384 for every i. Row k of m_old and v_old holds its span in its first old_bounds[k+1] - old_bounds[k] slots; later slots are unused. Some span has exactly 65536 entries in every draw.
All inputs are finite; a program needn't handle non-finite values.
Results may differ from a plain program's by a relative error of at most 0.0049.
Values may be sent and summed in bfloat16 or wider, within the bound.
A program may use at most 128 MiB of HBM per device.

v0:
```python
import jax
import jax.numpy as jnp
from jax import lax
from jax.sharding import Mesh
from jax.sharding import PartitionSpec as P

DP = ("dp_0", "dp_1", "dp_2", "dp_3")


def one_axis_at_a_time(array, axes):
    for axis in axes:
        array = lax.psum(array, axis)
    return array


def shifted(value, axis, steps):
    count = lax.axis_size(axis)
    leading, last = (max(0, -steps), min(count, count - steps))
    return lax.ppermute(value, axis, [(source, source + steps) for source in range(leading, last)])


def window(buffer, offset, width):
    padded = jnp.pad(buffer, ((0, 0), (2 * width, width)))
    return lax.dynamic_slice_in_dim(padded, offset + 2 * width, width, 1)


def local(grads, master, m_old, v_old, old_bounds):
    count = lax.axis_size(DP)
    device = lax.axis_index(DP)
    width = master.shape[0]
    local_grad = grads[0]
    gradient = lax.psum_scatter(local_grad, DP, scatter_dimension=0, tiled=True)
    total = one_axis_at_a_time(jnp.sum(gradient * gradient), DP)
    packed = jnp.stack([m_old[0], v_old[0]])
    from_before = shifted(packed.astype(jnp.bfloat16), DP, 1).astype(packed.dtype)
    from_after = shifted(packed.astype(jnp.bfloat16), DP, -1).astype(packed.dtype)
    start = device * width
    bound_before = old_bounds[jnp.maximum(device - 1, 0)]
    bound_here = old_bounds[device]
    bound_after = old_bounds[device + 1]
    part_before = window(from_before, start - bound_before, width)
    part_here = window(packed, start - bound_here, width)
    part_after = window(from_after, start - bound_after, width)
    positions = start + jnp.arange(width, dtype=jnp.int32)
    moments = jnp.where(
        positions[None, :] < bound_here,
        part_before,
        jnp.where(positions[None, :] >= bound_after, part_after, part_here),
    )
    m_prev = moments[0]
    v_prev = moments[1]
    clip = jnp.minimum(1.0, jnp.sqrt(jnp.float32(count * width)) / (jnp.sqrt(total) + 1e-06))
    clipped = clip * gradient
    m_new = 0.5 * m_prev + 0.5 * clipped
    v_new = 0.95 * v_prev + 0.05 * clipped * clipped
    direction = m_new / (1.0 - 0.5**20) / (jnp.sqrt(v_new / (1.0 - 0.95**20)) + 1e-08)
    master_new = master - 0.05 * (direction + 0.1 * master)
    params_full = lax.all_gather(master_new.astype(jnp.bfloat16), DP, axis=0, tiled=True)
    return (master_new, m_new, v_new, params_full)


def solution(mesh):
    finer = Mesh(mesh.devices.reshape(4, 4, 4, 2), ("dp_0", "dp_1", "dp_2", "dp_3"))
    placed = (P(DP, None), P(DP), P(DP, None), P(DP, None), P())
    return jax.shard_map(
        local, mesh=finer, in_specs=placed, out_specs=(P(DP), P(DP), P(DP), P()), check_vma=False
    )
```

profile of v0, /device:TPU:1, one launch (start us, length us, event | category | flops | bytes accessed | tf_op | source)
XLA Modules:
  0.0 352.3 jit_solution(15262826683552857965)
XLA Ops:
  7.2 0.0 copy-start.1
  7.2 0.0 copy-start
  7.2 0.0 copy-start.3
  7.2 0.0 copy-start.2
  7.2 0.0 all-reduce.6.cloned.1.call-start
  7.3 0.7 all-reduce.6.cloned.1.call-update
  7.9 0.0 all-gather.2.cloned.1.call-start
  8.0 0.1 copy-done.1
  8.1 0.1 copy-done
  8.2 0.5 fusion.5
  8.7 4.5 %collective-permute-start = (bf16[2,65536]{1,0:T(2,128)(2,1)S(1)}, bf16[2,65536]{1,0:T(2,128)(2,1)S(1)}, u32[]{:S(2)}, u32[]{:S(2)}) collective-permute-start(bf16[2,65536]{1,0:T(2,128)(2,1)S(1)} %fusion.5), channel_id=1, source_target_pairs={{0,1},{1,2},{2,3},{3,4},{4,5},{5,6},{6,7},{7,8},{8,9},{9,10},{10,1... | collective-permute-start | bytes 786440 | tf_op jit(solution)/shard_map/ppermute | solution.py:19
  13.2 1.9 collective-permute-start.1
  15.1 0.0 copy-done.3
  15.1 0.6 fusion.8
  17.7 0.5 pad_maximum_fusion
  18.2 1.3 fusion.3
  19.5 213.1 %all-reduce.6.cloned.1.call-done = f32[4194304]{0:T(1024)} async-done(((f32[4194304]{0:T(1024)}), f32[4194304]{0:T(1024)}) %all-reduce.6.cloned.1.call-update) | async-done | bytes 16777232
  232.6 1.5 multiply_reduce_fusion
  234.2 8.7 %psum.28 = f32[]{:T(128)} all-reduce(f32[]{:T(128)} %multiply_reduce_fusion), channel_id=1, replica_groups=mesh['dp_0'=4,'dp_1'=4,'dp_2'=4,'dp_3'=2] {'dp_0'}, use_global_device_ids=true, to_apply=%region_2.0 | all-reduce | flops 1 | bytes 8 | tf_op jit(solution)/shard_map/psum | solution.py:12
  242.8 8.5 %psum.29 = f32[]{:T(128)} all-reduce(f32[]{:T(128)} %psum.28), channel_id=1, replica_groups=mesh['dp_0'=4,'dp_1'=4,'dp_2'=4,'dp_3'=2] {'dp_1'}, use_global_device_ids=true, to_apply=%region_3.0 | all-reduce | flops 1 | bytes 8 | tf_op jit(solution)/shard_map/psum | solution.py:12
  251.3 0.0 collective-permute-done
  251.3 0.0 collective-permute-done.1
  251.3 2.1 fusion.1
  253.4 7.9 %psum.30 = f32[]{:T(128)} all-reduce(f32[]{:T(128)} %psum.29), channel_id=1, replica_groups=mesh['dp_0'=4,'dp_1'=4,'dp_2'=4,'dp_3'=2] {'dp_2'}, use_global_device_ids=true, to_apply=%region_4.0 | all-reduce | flops 1 | bytes 8 | tf_op jit(solution)/shard_map/psum | solution.py:12
  261.4 0.2 slice_multiply_fusion
  261.6 8.7 %psum.31 = f32[]{:T(128)} all-reduce(f32[]{:T(128)} %psum.30), channel_id=1, replica_groups=mesh['dp_0'=4,'dp_1'=4,'dp_2'=4,'dp_3'=2] {'dp_3'}, use_global_device_ids=true, to_apply=%region_5.0 | all-reduce | flops 1 | bytes 8 | tf_op jit(solution)/shard_map/psum | solution.py:12
  271.0 0.0 copy-done.2
  271.0 1.8 fusion.6
  272.8 0.0 all-gather.2.cloned.1.call-update
  272.8 65.5 %all-gather.2.cloned.1.call-done = bf16[4194304]{0:T(1024)(128)(2,1)} async-done(((bf16[32768]{0:T(1024)(128)(2,1)}), bf16[4194304]{0:T(1024)(128)(2,1)}) %all-gather.2.cloned.1.call-update) | async-done | bytes 8388624 | tf_op jit(solution)/shard_map/all_gather | solution.py:58
  338.3 7.1 %copy.12 = bf16[4194304]{0:T(1024)(128)(2,1)} copy(bf16[4194304]{0:T(1024)(128)(2,1)} %all-gather.2.cloned.1.call-done) | data formatting | bytes 16777216
Async XLA Ops:
  7.2 1.0 copy-start.1
  7.2 1.0 copy-start
  7.2 7.9 %copy-start.3 = (s32[129]{0:T(256)S(1)}, s32[129]{0:T(256)}, u32[]{:S(2)}) copy-start(s32[129]{0:T(256)} %param.9) | copy-start | bytes 1552
  7.2 263.8 %copy-start.2 = (f32[32768]{0:T(1024)S(1)}, f32[32768]{0:T(1024)}, u32[]{:S(2)}) copy-start(f32[32768]{0:T(1024)} %param.6) | copy-start | bytes 393220
  7.2 225.4 %all-reduce.6.cloned.1.call-start = ((), (), s32[]{:S(2)}) async-start(), calls=%async_computation.1 | async-start | bytes 33554432
  7.9 330.4 %all-gather.2.cloned.1.call-start = ((), (), s32[]{:S(2)}) async-start(), calls=%async_computation | async-start | bytes 8454144 | tf_op jit(solution)/shard_map/all_gather | solution.py:58
  8.7 242.7 %collective-permute-start = (bf16[2,65536]{1,0:T(2,128)(2,1)S(1)}, bf16[2,65536]{1,0:T(2,128)(2,1)S(1)}, u32[]{:S(2)}, u32[]{:S(2)}) collective-permute-start(bf16[2,65536]{1,0:T(2,128)(2,1)S(1)} %fusion.5), channel_id=1, source_target_pairs={{0,1},{1,2},{2,3},{3,4},{4,5},{5,6},{6,7},{7,8},{8,9},{9,10},{10,1... | collective-permute-start | bytes 786440 | tf_op jit(solution)/shard_map/ppermute | solution.py:19
  13.2 238.2 %collective-permute-start.1 = (bf16[2,65536]{1,0:T(2,128)(2,1)S(1)}, bf16[2,65536]{1,0:T(2,128)(2,1)S(1)}, u32[]{:S(2)}, u32[]{:S(2)}) collective-permute-start(bf16[2,65536]{1,0:T(2,128)(2,1)S(1)} %fusion.5), channel_id=1, source_target_pairs={{1,0},{2,1},{3,2},{4,3},{5,4},{6,5},{7,6},{8,7},{9,8},{10,9},{11,1... | collective-permute-start | bytes 786440 | tf_op jit(solution)/shard_map/ppermute | solution.py:19
Sparse Core Ops, SparseCore 0:
  13.4 219.1 all-reduce.5
  272.9 65.3 all-gather.1
where the time goes:
time: 353 us; the launch traced here: 352 us
  waiting for transfers between devices  279 us (79%)
  blocking collectives  33.8 us (10%)
  between operations  16.8 us (5%)
  other arithmetic  7.93 us (2%)
  local copies, waits for them, and re-layouts  7.92 us (2%)
  starting transfers between devices  6.49 us (2%)
    unnamed x3, waiting for transfers between devices  214 us
    all_gather x1, waiting for transfers between devices, local(): lax.all_gather(master_new.astype(jnp.bfloat16), DP, axis=0, tiled=True)  65.5 us
    psum x4, blocking collectives, one_axis_at_a_time(): array = lax.psum(array, axis)  33.8 us
    unnamed x9, local copies, waits for them, and re-layouts  7.33 us
  transfers between devices with their start and end apart: 4, of which 2 were waited for; matrix products, arithmetic and copies ran while one was open for 1% of the time, Pallas kernels for 0%

commit v1 on v0

v1 whole, which is shorter than its diff:
```python
import jax
import jax.numpy as jnp
from jax import lax
from jax.experimental import pallas as pl
from jax.experimental.pallas import tpu as pltpu
from jax.sharding import Mesh
from jax.sharding import PartitionSpec as P

DP = ("dz", "dy", "dx", "dc")
F32, BF16 = jnp.float32, jnp.bfloat16
LANES = 128
ORDERS = ((2, 1, 0), (1, 0, 2), (0, 2, 1))
HALVES = ((48, 48), (48, 48), (32, 32))
SLOTS = (2, 1, 3, 0)
FAR, DIRECT, RELAY = 0, 1, 2


def plan(rows):
    spans, at = [], 0
    for pair in HALVES:
        colour = []
        for part in pair:
            size = part * rows // 256
            colour.append((at, size))
            at += size
        spans.append(colour)
    return spans


def kernel(spans, rows, refs):
    g, master, window, tail, head, bounds = refs["in"]
    master_out, m_out, v_out, params = refs["out"]
    s = refs["scratch"]
    coords = [lax.axis_index(name) for name in DP[:3]]
    core = lax.axis_index("dc")
    other = 1 - core
    me = ((coords[0] * 4 + coords[1]) * 4 + coords[2]) * 2 + core

    def moved(dim, steps):
        at = list(coords)
        at[dim] = (coords[dim] + steps + 4) % 4
        return (*at, core)

    def located(index):
        return (index // 32, (index // 8) % 4, (index // 2) % 4, index % 2)

    partner = (*coords, other)
    after, before = located((me + 1) % 128), located((me + 127) % 128)
    beside = located((me + 127 + 2 * core) % 128)

    def remote(src, dst, send, recv, device):
        return pltpu.make_async_remote_copy(
            src_ref=src, dst_ref=dst, send_sem=send, recv_sem=recv, device_id=device, device_id_type=pl.DeviceIdType.MESH
        )

    def source(k, slot, parity):
        first = ORDERS[k][0]
        at = [slice(None)] * 3
        at[first] = (coords[first] + slot) % 4
        low = spans[k][0][0]
        size = spans[k][0][1] + spans[k][1][1]
        return g.at[at[0], at[1], at[2], parity, pl.ds(low, size)]

    loads = {}
    for slot in SLOTS:
        for k in range(3):
            loads[k, slot, 1] = pltpu.make_async_copy(source(k, slot, other), s["theirs"][k].at[slot], s["load"].at[k, slot, 1])
            loads[k, slot, 0] = pltpu.make_async_copy(source(k, slot, core), s["ours"][k].at[slot], s["load"].at[k, slot, 0])
            loads[k, slot, 1].start()
            loads[k, slot, 0].start()
    small = [
        pltpu.make_async_copy(master, s["master"], s["small"].at[0]),
        pltpu.make_async_copy(window, s["window"], s["small"].at[1]),
    ]
    for copy in small:
        copy.start()

    barrier = pltpu.get_barrier_semaphore()
    peers = [moved(dim, step) for dim in range(3) for step in (1, 2, 3)] + [partner, beside]
    for peer in peers:
        pl.semaphore_signal(barrier, inc=1, device_id=peer, device_id_type=pl.DeviceIdType.MESH)
    pl.semaphore_wait(barrier, len(peers))

    pending = []

    def launch(copy):
        copy.start()
        pending.append(copy)
        return copy

    swaps = {}
    for slot in range(4):
        for k in range(3):
            swaps[k, slot] = remote(
                s["give"][k].at[slot], s["take"][k].at[slot], s["swap_out"].at[k, slot], s["swap_in"].at[k, slot], partner
            )

    def narrow(k, slot):
        loads[k, slot, 1].wait()

        def body(t, carry):
            s["give"][k][slot, t // 4, t % 4] = s["theirs"][k][slot, t // 4, t % 4].astype(BF16)
            return carry

        lax.fori_loop(0, 16, body, 0)
        launch(swaps[k, slot])

    def joined(k, slot, h, t):
        u, v = (t // 4, t % 4) if ORDERS[k][1] < ORDERS[k][2] else (t % 4, t // 4)
        low = spans[k][h][0] - spans[k][0][0]
        at = pl.ds(low, spans[k][h][1])
        return s["ours"][k][slot, u, v, at] + s["take"][k][slot, u, v, at].astype(F32)

    def arrive(k, slot):
        loads[k, slot, 0].wait()
        swaps[k, slot].wait_recv()

    streams = [(k, h) for k in range(3) for h in range(2)]
    sign = {0: 1, 1: -1}

    rs = {}
    for q, (k, h) in enumerate(streams):
        for phase in range(3):
            dim = ORDERS[k][phase]
            for kind, step in ((FAR, sign[h]), (DIRECT, -sign[h]), (RELAY, sign[h])):
                rs[q, phase, kind] = remote(
                    s["out"][q][phase].at[kind],
                    s["in"][q][phase].at[kind],
                    s["rs_out"].at[q, phase, kind],
                    s["rs_in"].at[q, phase, kind],
                    moved(dim, step),
                )

    def loop(count, body):
        def step(t, carry):
            body(t)
            return carry

        lax.fori_loop(0, count, step, 0)

    for k in range(3):
        narrow(k, 2)
    for k in range(3):
        narrow(k, 3)
        arrive(k, 2)
        for h in range(2):
            q = 2 * k + h

            def body(t, k=k, h=h, q=q):
                s["out"][q][0][FAR, t] = joined(k, 2, h, t).astype(BF16)

            loop(16, body)
            launch(rs[q, 0, FAR])
    for k in range(3):
        narrow(k, 1)
    for h, slot in ((0, 3), (1, 1)):
        for k in range(3):
            q = 2 * k + h
            arrive(k, slot)

            def body(t, k=k, h=h, q=q, slot=slot):
                s["out"][q][0][DIRECT, t] = joined(k, slot, h, t).astype(BF16)

            loop(16, body)
            launch(rs[q, 0, DIRECT])
    for k in range(3):
        narrow(k, 0)
    moments_out = [
        launch(remote(tail, s["from_before"], s["mom_out"].at[0], s["mom_in"].at[0], after)),
        launch(remote(head, s["from_after"], s["mom_out"].at[1], s["mom_in"].at[1], before)),
    ]
    for q, (k, h) in enumerate(streams):
        rs[q, 0, FAR].wait_recv()

        def body(t, k=k, h=h, q=q):
            value = joined(k, sign[h] % 4, h, t) + s["in"][q][0][FAR, t].astype(F32)
            s["out"][q][0][RELAY, t] = value.astype(BF16)

        loop(16, body)
        launch(rs[q, 0, RELAY])

    for copy in small:
        copy.wait()
    for copy in moments_out:
        copy.wait_recv()
    start = me * (rows * LANES)
    low, high = bounds[me] - start, bounds[me + 1] - start
    place = lax.broadcasted_iota(jnp.int32, (rows // 2, LANES), 0) * LANES + lax.broadcasted_iota(
        jnp.int32, (rows // 2, LANES), 1
    )
    for i in range(2):
        top, bottom = pl.ds(0, rows // 2), pl.ds(rows // 2, rows // 2)
        s["window"][i, top] = jnp.where(place < low, s["from_before"][i].astype(F32), s["window"][i, top])
        s["window"][i, bottom] = jnp.where(
            place + (rows // 2) * LANES >= high, s["from_after"][i].astype(F32), s["window"][i, bottom]
        )

    for k in range(3):
        arrive(k, 0)
    for q, (k, h) in enumerate(streams):
        rs[q, 0, DIRECT].wait_recv()
        rs[q, 0, RELAY].wait_recv()

        def body(t, k=k, h=h, q=q):
            got = s["in"][q][0]
            s["sum"][q][0][t] = joined(k, 0, h, t) + got[DIRECT, t].astype(F32) + got[RELAY, t].astype(F32)

        loop(16, body)
        if True:
            second(s, rs, launch, loop, coords, q, k, h, sign, 1, 4)
    for q, (k, h) in enumerate(streams):
        relay(s, rs, launch, loop, coords, q, k, h, sign, 1, 4)
    for q, (k, h) in enumerate(streams):
        finish(s, rs, loop, coords, q, k, 1, 4)
        second(s, rs, launch, loop, coords, q, k, h, sign, 2, 1)
    for q, (k, h) in enumerate(streams):
        relay(s, rs, launch, loop, coords, q, k, h, sign, 2, 1)
    total = jnp.zeros((8, LANES), F32)
    for q, (k, h) in enumerate(streams):
        finish(s, rs, loop, coords, q, k, 2, 1)
        value = s["sum"][q][2][0]
        square = value * value
        for i in range(spans[k][h][1] // 8):
            total += square[8 * i : 8 * i + 8]

    s["norm"][0] = total
    copy = launch(remote(s["norm"].at[0], s["norm_in"].at[0], s["norm_out"].at[0], s["norm_got"].at[0], partner))
    copy.wait_recv()
    s["norm"][1] = s["norm"][0] + s["norm_in"][0]
    for dim in range(3):
        copies = [
            launch(
                remote(
                    s["norm"].at[1 + dim],
                    s["norm_in"].at[3 * dim + step],
                    s["norm_out"].at[3 * dim + step],
                    s["norm_got"].at[3 * dim + step],
                    moved(dim, step),
                )
            )
            for step in (1, 2, 3)
        ]
        value = s["norm"][1 + dim]
        for step, copy in zip((1, 2, 3), copies):
            copy.wait_recv()
            value += s["norm_in"][3 * dim + step]
        s["norm"][2 + dim] = value
    norm = jnp.sum(s["norm"][4], axis=(0, 1), keepdims=True)
    clip = jnp.minimum(1.0, jnp.sqrt(F32(128 * rows * LANES)) / (jnp.sqrt(norm) + 1e-06))

    for q, (k, h) in enumerate(streams):
        at = pl.ds(*spans[k][h])
        clipped = clip * s["sum"][q][2][0]
        m_new = 0.5 * s["window"][0, at] + 0.5 * clipped
        v_new = 0.95 * s["window"][1, at] + 0.05 * clipped * clipped
        direction = m_new / (1.0 - 0.5**20) / (jnp.sqrt(v_new / (1.0 - 0.95**20)) + 1e-08)
        weights = s["master"][at]
        weights = weights - 0.05 * (direction + 0.1 * weights)
        master_out[at] = weights
        m_out[at] = m_new
        v_out[at] = v_new
        params[coords[0], coords[1], coords[2], core, at] = weights.astype(BF16)

    def piece(k, fixed, low, size):
        at = [fixed.get(dim, slice(None)) for dim in range(3)]
        return params.at[at[0], at[1], at[2], core, pl.ds(low, size)]

    def fixed_at(k, stage, step):
        order = ORDERS[k][::-1]
        fixed = {dim: coords[dim] for dim in order[stage:]}
        fixed[order[stage]] = (coords[order[stage]] + step + 4) % 4
        return fixed

    def sent(ref, sem, device):
        return remote(ref, ref, s["ag_out"].at[sem], s["ag_in"].at[sem], device)

    def sem_of(k, stage, i):
        return (k * 3 + stage) * 4 + i

    shared = []

    def share(k, stage, step):
        low = spans[k][0][0]
        size = spans[k][0][1] + spans[k][1][1]
        i = len(shared)
        ref = piece(k, fixed_at(k, stage, step), low, size)
        shared.append(launch(remote(ref, ref, s["share_out"].at[i], s["share_in"].at[i], partner)))

    for k in range(3):
        share(k, 0, 0)
    for stage in range(3):
        hops = {}
        for k in range(3):
            dim = ORDERS[k][::-1][stage]
            low, size = spans[k][0][0], spans[k][0][1] + spans[k][1][1]
            ref = piece(k, fixed_at(k, stage, 0), low, size)
            for i, step in ((0, 1), (1, -1)):
                hops[k, i] = launch(sent(ref, sem_of(k, stage, i), moved(dim, step)))
        for k in range(3):
            dim = ORDERS[k][::-1][stage]
            for i, step in ((0, 1), (1, -1)):
                hops[k, i].wait_recv()
                ref = piece(k, fixed_at(k, stage, -step), *spans[k][i])
                hops[k, 2 + i] = launch(sent(ref, sem_of(k, stage, 2 + i), moved(dim, step)))
                share(k, stage, -step)
        for k in range(3):
            hops[k, 2].wait_recv()
            hops[k, 3].wait_recv()
            share(k, stage, 2)
    for copy in shared:
        copy.wait_recv()
    for copy in pending:
        copy.wait_send()


def second(s, rs, launch, loop, coords, q, k, h, sign, phase, count):
    place = coords[ORDERS[k][phase]]
    for kind, step in ((FAR, 2), (DIRECT, -sign[h])):
        at = ((place + step + 4) % 4) * count

        def body(t, kind=kind, at=at):
            s["out"][q][phase][kind, t] = s["sum"][q][phase - 1][at + t].astype(BF16)

        loop(count, body)
        launch(rs[q, phase, kind])


def relay(s, rs, launch, loop, coords, q, k, h, sign, phase, count):
    place = coords[ORDERS[k][phase]]
    rs[q, phase, FAR].wait_recv()
    at = ((place + sign[h] + 4) % 4) * count

    def body(t):
        value = s["sum"][q][phase - 1][at + t] + s["in"][q][phase][FAR, t].astype(F32)
        s["out"][q][phase][RELAY, t] = value.astype(BF16)

    loop(count, body)
    launch(rs[q, phase, RELAY])


def finish(s, rs, loop, coords, q, k, phase, count):
    place = coords[ORDERS[k][phase]]
    rs[q, phase, DIRECT].wait_recv()
    rs[q, phase, RELAY].wait_recv()
    at = place * count

    def body(t):
        got = s["in"][q][phase]
        s["sum"][q][phase][t] = s["sum"][q][phase - 1][at + t] + got[DIRECT, t].astype(F32) + got[RELAY, t].astype(F32)

    loop(count, body)


def step(g, master, window, tail, head, bounds):
    rows = master.shape[0]
    spans = plan(rows)
    sizes = [a[1] + b[1] for a, b in spans]
    dma = pltpu.SemaphoreType.DMA
    halves = [span for colour in spans for span in colour]
    scratch = {
        "theirs": [pltpu.VMEM((4, 4, 4, n, LANES), F32) for n in sizes],
        "ours": [pltpu.VMEM((4, 4, 4, n, LANES), F32) for n in sizes],
        "give": [pltpu.VMEM((4, 4, 4, n, LANES), BF16) for n in sizes],
        "take": [pltpu.VMEM((4, 4, 4, n, LANES), BF16) for n in sizes],
        "out": [[pltpu.VMEM((3, m, n, LANES), BF16) for m in (16, 4, 1)] for _, n in halves],
        "in": [[pltpu.VMEM((3, m, n, LANES), BF16) for m in (16, 4, 1)] for _, n in halves],
        "sum": [[pltpu.VMEM((m, n, LANES), F32) for m in (16, 4, 1)] for _, n in halves],
        "master": pltpu.VMEM((rows, LANES), F32),
        "window": pltpu.VMEM((2, rows, LANES), F32),
        "from_before": pltpu.VMEM((2, rows // 2, LANES), BF16),
        "from_after": pltpu.VMEM((2, rows // 2, LANES), BF16),
        "norm": pltpu.VMEM((5, 8, LANES), F32),
        "norm_in": pltpu.VMEM((10, 8, LANES), F32),
        "load": dma((3, 4, 2)),
        "small": dma((2,)),
        "swap_out": dma((3, 4)),
        "swap_in": dma((3, 4)),
        "rs_out": dma((6, 3, 3)),
        "rs_in": dma((6, 3, 3)),
        "mom_out": dma((2,)),
        "mom_in": dma((2,)),
        "norm_out": dma((10,)),
        "norm_got": dma((10,)),
        "ag_out": dma((36,)),
        "ag_in": dma((36,)),
        "share_out": dma((30,)),
        "share_in": dma((30,)),
    }
    leaves, tree = jax.tree.flatten(scratch)

    def body(*refs):
        kernel(
            spans,
            rows,
            {"in": refs[:6], "out": refs[6:10], "scratch": jax.tree.unflatten(tree, refs[10:])},
        )

    whole = pl.BlockSpec(memory_space=pl.ANY)
    vmem = pl.BlockSpec(memory_space=pltpu.VMEM)
    return pl.pallas_call(
        body,
        name="adam_step",
        out_shape=(
            jax.ShapeDtypeStruct((rows, LANES), F32),
            jax.ShapeDtypeStruct((rows, LANES), F32),
            jax.ShapeDtypeStruct((rows, LANES), F32),
            jax.ShapeDtypeStruct((4, 4, 4, 2, rows, LANES), BF16),
        ),
        in_specs=[whole] * 5 + [pl.BlockSpec(memory_space=pltpu.SMEM)],
        out_specs=[vmem] * 4,
        scratch_shapes=leaves,
        compiler_params=pltpu.CompilerParams(collective_id=0, has_side_effects=True, vmem_limit_bytes=67_000_000),
    )(g, master, window, tail, head, bounds)


def local(grads, master, m_old, v_old, old_bounds):
    width = master.shape[0]
    rows, half = width // LANES, width // 2
    device = lax.axis_index(DP)
    begin = device * width - old_bounds[device]
    packed = jnp.concatenate([m_old, v_old])
    padded = jnp.pad(packed, ((0, 0), (width, 0)))

    def cut(offset, size):
        return lax.dynamic_slice_in_dim(padded, offset + width, size, 1).reshape(2, size // LANES, LANES)

    window = cut(begin, width)
    tail = cut(begin + width, half).astype(BF16)
    head = cut(begin - half, half).astype(BF16)
    master_new, m_new, v_new, params = step(
        grads.reshape(4, 4, 4, 2, rows, LANES), master.reshape(rows, LANES), window, tail, head, old_bounds
    )
    return master_new.reshape(width), m_new.reshape(width), v_new.reshape(width), params.reshape(128 * width)


def solution(mesh):
    finer = Mesh(mesh.devices.reshape(4, 4, 4, 2), DP)
    placed = (P(DP, None), P(DP), P(DP, None), P(DP, None), P())
    return jax.shard_map(local, mesh=finer, in_specs=placed, out_specs=(P(DP), P(DP), P(DP), P()), check_vma=False)
```

time: 353 us -> 110 us (0.31)
  waiting for transfers between devices: 279 us -> 0 us
  Pallas kernels: 0 us -> 91.6 us
  blocking collectives: 33.8 us -> 0 us
  between operations: 16.8 us -> 1.34 us
  local copies, waits for them, and re-layouts: 7.92 us -> 15 us
  starting transfers between devices: 6.49 us -> 0 us
  other arithmetic: 7.93 us -> 1.56 us
    unnamed x3 -> x0, waiting for transfers between devices: 214 us -> none
    pallas_call x0 -> x1, Pallas kernels: none -> 91.6 us  [step(): pl.pallas_call(body, name='adam_step', out_shape=(jax.ShapeDtypeStruct((r...]
    all_gather x1 -> x0, waiting for transfers between devices: 65.5 us -> none  [local(): lax.all_gather(master_new.astype(jnp.bfloat16), DP, axis=0, tiled=True)]
    psum x4 -> x0, blocking collectives: 33.8 us -> none  [one_axis_at_a_time(): array = lax.psum(array, axis)]
    ppermute x2 -> x0, starting transfers between devices: 6.42 us -> none  [shifted(): lax.ppermute(value, axis, [(source, source + steps) for source in range(l...]
    unnamed x9 -> x7, local copies, waits for them, and re-layouts: 7.33 us -> 13.1 us
  transfers between devices with their start and end apart: 4 -> 0, of which waited for: 2 -> 0; matrix products, arithmetic and copies ran while one was open for 1% -> 0% of each run, Pallas kernels for 0% -> 0%
where the time goes in v1:
time: 110 us
  Pallas kernels  91.6 us (83%)
  local copies, waits for them, and re-layouts  15 us (14%)
  other arithmetic  1.56 us (1%)
  between operations  1.34 us (1%)
    pallas_call x1, Pallas kernels, step(): pl.pallas_call(body, name='adam_step', out_shape=(jax.ShapeDtypeStruct((r...  91.6 us
    unnamed x7, local copies, waits for them, and re-layouts  13.1 us

profile of v1, /device:TPU:1, one launch (start us, length us, event | category | flops | bytes accessed | tf_op | source)
XLA Modules:
  0.0 109.5 jit_solution(7955611454040868018)
XLA Ops:
  0.6 1.3 %dynamic_slice.12 = s32[1]{0:T(128)} dynamic-slice(s32[129]{0:T(256)} %refs_5_.1, s32[]{:T(128)S(6)} %select_n.12), dynamic_slice_sizes={1} | dynamic-slice | bytes 12 | tf_op jit(solution)/shard_map/dynamic_slice | solution.py:420
  2.6 1.6 %select_maximum_fusion = f32[2,98304]{1,0:T(2,128)S(1)} fusion(f32[1,65536]{1,0:T(1,128)} %param.8, f32[1,65536]{1,0:T(1,128)} %param.7), kind=kLoop, calls=%fused_computation | loop fusion | flops 786432 | bytes 1310720 | tf_op jit(solution)/shard_map/concatenate | solution.py:421
  4.1 0.2 fusion.1
  4.4 0.3 dynamic-slice_bitcast_fusion
  4.7 0.7 copy.15
  5.4 0.7 copy_bitcast_fusion.1
  6.1 91.6 %adam_step.1 = (f32[256,128]{1,0:T(8,128)}, f32[256,128]{1,0:T(8,128)}, f32[256,128]{1,0:T(8,128)}, bf16[4,4,4,2,256,128]{5,4,3,2,1,0:T(8,128)(2,1)}) custom-call(f32[4,4,4,2,256,128]{5,4,3,2,1,0:T(8,128)} %bitcast.20, f32[256,128]{1,0:T(8,128)} %bitcast.23, f32[2,256,128]{2,1,0:T(8,128)} %bitcast.22, bf16[2,128,128]{2,1,0:T(8,128)(2,1)} %get-tuple-element.15.refs_3_, ...), custom_call_target="tpu_custom_call" | custom-call | tf_op jit(solution)/shard_map/adam_step/pallas_call | solution.py:400
  97.7 1.6 %copy.20 = f32[32768]{0:T(1024)} copy(f32[32768]{0:T(1024)} %bitcast.26) | data formatting | bytes 262144
  99.3 1.6 %copy.21 = f32[32768]{0:T(1024)} copy(f32[32768]{0:T(1024)} %bitcast.25) | data formatting | bytes 262144
  100.8 1.6 %copy.22 = f32[32768]{0:T(1024)} copy(f32[32768]{0:T(1024)} %bitcast.24) | data formatting | bytes 262144
  102.4 7.1 %copy.23 = bf16[4194304]{0:T(1024)(128)(2,1)} copy(bf16[4194304]{0:T(1024)(128)(2,1)} %bitcast.21) | data formatting | bytes 16777216

commit v2 on v1

v2 whole, which is shorter than its diff:
```python
import jax
import jax.numpy as jnp
from jax import lax
from jax.experimental import pallas as pl
from jax.experimental.pallas import tpu as pltpu
from jax.sharding import Mesh
from jax.sharding import PartitionSpec as P

DP = ("dz", "dy", "dx", "dc")
F32, BF16 = jnp.float32, jnp.bfloat16
LANES = 128
CUT = 64
ORDERS = ((2, 1, 0), (1, 0, 2), (0, 2, 1))
HALVES = ((48, 40), (48, 40), (40, 40))
SLOTS = (2, 1, 3, 0)
FAR, DIRECT, RELAY = 0, 1, 2


def plan(rows):
    spans, at = [], 0
    for pair in HALVES:
        colour = []
        for part in pair:
            size = part * rows // 256
            colour.append((at, size))
            at += size
        spans.append(colour)
    return spans


def kernel(spans, rows, refs):
    g, master, m_old, v_old, bounds = refs["in"]
    master_out, m_out, v_out, params = refs["out"]
    s = refs["scratch"]
    coords = [lax.axis_index(name) for name in DP[:3]]
    core = lax.axis_index("dc")
    other = 1 - core
    me = ((coords[0] * 4 + coords[1]) * 4 + coords[2]) * 2 + core

    def moved(dim, steps):
        at = list(coords)
        at[dim] = (coords[dim] + steps + 4) % 4
        return (*at, core)

    def located(index):
        return (index // 32, (index // 8) % 4, (index // 2) % 4, index % 2)

    partner = (*coords, other)
    after, before = located((me + 1) % 128), located((me + 127) % 128)
    beside = located((me + 127 + 2 * core) % 128)

    def remote(src, dst, send, recv, device):
        return pltpu.make_async_remote_copy(
            src_ref=src, dst_ref=dst, send_sem=send, recv_sem=recv, device_id=device, device_id_type=pl.DeviceIdType.MESH
        )

    def source(k, slot, parity):
        first = ORDERS[k][0]
        at = [slice(None)] * 3
        at[first] = (coords[first] + slot) % 4
        low = spans[k][0][0]
        size = spans[k][0][1] + spans[k][1][1]
        return g.at[at[0], at[1], at[2], parity, pl.ds(low, size)]

    loads = {}
    for slot in SLOTS:
        for k in range(3):
            loads[k, slot, 1] = pltpu.make_async_copy(source(k, slot, other), s["theirs"][k].at[slot], s["load"].at[k, slot, 1])
            loads[k, slot, 0] = pltpu.make_async_copy(source(k, slot, core), s["ours"][k].at[slot], s["load"].at[k, slot, 0])
            loads[k, slot, 1].start()
            loads[k, slot, 0].start()
    small = [
        pltpu.make_async_copy(master, s["master"], s["small"].at[0]),
        pltpu.make_async_copy(m_old, s["old"].at[0, pl.ds(rows, 2 * rows)], s["small"].at[1]),
        pltpu.make_async_copy(v_old, s["old"].at[1, pl.ds(rows, 2 * rows)], s["small"].at[1]),
    ]
    for copy in small:
        copy.start()

    barrier = pltpu.get_barrier_semaphore()
    peers = [moved(dim, step) for dim in range(3) for step in (1, 2, 3)] + [partner, beside]
    for peer in peers:
        pl.semaphore_signal(barrier, inc=1, device_id=peer, device_id_type=pl.DeviceIdType.MESH)
    pl.semaphore_wait(barrier, len(peers))

    def launch(copy):
        copy.start()
        return copy

    def settled(ref, sem):
        pltpu.make_async_copy(ref, ref, sem).wait()

    swaps = {}
    for slot in range(4):
        for k in range(3):
            swaps[k, slot] = remote(
                s["give"][k].at[slot], s["take"][k].at[slot], s["sent"].at[0], s["swap_in"].at[k, slot], partner
            )

    def narrow(k, slot):
        loads[k, slot, 1].wait()

        def body(t, carry):
            s["give"][k][slot, t // 4, t % 4] = s["theirs"][k][slot, t // 4, t % 4].astype(BF16)
            return carry

        lax.fori_loop(0, 16, body, 0)
        launch(swaps[k, slot])

    def joined(k, slot, h, t):
        u, v = (t // 4, t % 4) if ORDERS[k][1] < ORDERS[k][2] else (t % 4, t // 4)
        low = spans[k][h][0] - spans[k][0][0]
        at = pl.ds(low, spans[k][h][1])
        return s["ours"][k][slot, u, v, at] + s["take"][k][slot, u, v, at].astype(F32)

    def arrive(k, slot):
        loads[k, slot, 0].wait()
        swaps[k, slot].wait_recv()

    streams = [(k, h) for k in range(3) for h in range(2)]
    sign = {0: 1, 1: -1}

    def steps_of(h, phase):
        return ((FAR, 2 if phase == 2 else sign[h]), (DIRECT, -sign[h]), (RELAY, sign[h]))

    rs = {}
    for q, (k, h) in enumerate(streams):
        for phase in range(3):
            dim = ORDERS[k][phase]
            for kind, step in steps_of(h, phase):
                rs[q, phase, kind] = remote(
                    s["out"][q][phase].at[kind],
                    s["in"][q][phase].at[kind],
                    s["sent"].at[1 + phase],
                    s["rs_in"].at[q, phase, 0 if kind == FAR and phase < 2 else 1],
                    moved(dim, step),
                )

    def loop(count, body):
        def step(t, carry):
            body(t)
            return carry

        lax.fori_loop(0, count, step, 0)

    for k in range(3):
        narrow(k, 2)
    for k in range(3):
        narrow(k, 3)
        arrive(k, 2)
        for h in range(2):
            q = 2 * k + h

            def body(t, k=k, h=h, q=q):
                s["out"][q][0][FAR, t] = joined(k, 2, h, t).astype(BF16)

            loop(16, body)
            launch(rs[q, 0, FAR])
    for k in range(3):
        narrow(k, 1)
    for h, slot in ((0, 3), (1, 1)):
        for k in range(3):
            q = 2 * k + h
            arrive(k, slot)

            def body(t, k=k, h=h, q=q, slot=slot):
                s["out"][q][0][DIRECT, t] = joined(k, slot, h, t).astype(BF16)

            loop(16, body)
            launch(rs[q, 0, DIRECT])
    for k in range(3):
        narrow(k, 0)
    for q, (k, h) in enumerate(streams):
        rs[q, 0, FAR].wait_recv()

        def body(t, k=k, h=h, q=q):
            value = joined(k, sign[h] % 4, h, t) + s["in"][q][0][FAR, t].astype(F32)
            s["out"][q][0][RELAY, t] = value.astype(BF16)

        loop(16, body)
        launch(rs[q, 0, RELAY])

    moments_out = moments(s, rows, small, bounds, me, launch, remote, after, before)
    for k in range(3):
        arrive(k, 0)
    for q, (k, h) in enumerate(streams):
        settled(s["in"][q][0].at[pl.ds(DIRECT, 2)], s["rs_in"].at[q, 0, 1])

        def body(t, k=k, h=h, q=q):
            got = s["in"][q][0]
            s["sum"][q][0][t] = joined(k, 0, h, t) + got[DIRECT, t].astype(F32) + got[RELAY, t].astype(F32)

        loop(16, body)
        if True:
            second(s, rs, launch, loop, coords, q, k, h, sign, 1, 4)
    for q, (k, h) in enumerate(streams):
        relay(s, rs, launch, loop, coords, q, k, h, sign, 1, 4)
    for q, (k, h) in enumerate(streams):
        finish(s, rs, loop, coords, q, k, 1, 4)
        second(s, rs, launch, loop, coords, q, k, h, sign, 2, 1)
    total = jnp.zeros((8, LANES), F32)
    for q, (k, h) in enumerate(streams):
        finish(s, rs, loop, coords, q, k, 2, 1)
        value = s["sum"][q][2][0]
        square = value * value
        for i in range(spans[k][h][1] // 8):
            total += square[8 * i : 8 * i + 8]

    def merge():
        for copy in moments_out:
            copy.wait_recv()
        start = me * (rows * LANES)
        low, high = bounds[me] - start, bounds[me + 1] - start
        place = lax.broadcasted_iota(jnp.int32, (rows // 2, LANES), 0) * LANES + lax.broadcasted_iota(
            jnp.int32, (rows // 2, LANES), 1
        )
        for i in range(2):
            top, bottom = pl.ds(0, rows // 2), pl.ds(rows // 2, rows // 2)
            s["window"][i, top] = jnp.where(place < low, s["from_before"][i].astype(F32), s["window"][i, top])
            s["window"][i, bottom] = jnp.where(
                place + (rows // 2) * LANES >= high, s["from_after"][i].astype(F32), s["window"][i, bottom]
            )

    s["norm"][0] = jnp.sum(total, axis=0, keepdims=True)
    column = [(moved(0, step)[:3], c) for step in range(4) for c in (core, other)][1:]
    column = [(*place, c) for place, c in column]
    plane = [
        (coords[0], (coords[1] + y) % 4, (coords[2] + x) % 4, core) for y in range(4) for x in range(4)
    ][1:]
    for round_, group, base in ((0, column, 0), (1, plane, 7)):
        for i, device in enumerate(group):
            launch(
                remote(
                    s["norm"].at[round_],
                    s["norm_in"].at[base + i],
                    s["sent"].at[4],
                    s["norm_got"].at[round_],
                    device,
                )
            )
        value = s["norm"][round_]
        if round_ == 0:
            merge()
        settled(s["norm_in"].at[pl.ds(base, len(group))], s["norm_got"].at[round_])
        for i in range(len(group)):
            value += s["norm_in"][base + i]
        s["norm"][round_ + 1] = value
    norm = jnp.sum(s["norm"][2], axis=(0, 1), keepdims=True)
    clip = jnp.minimum(1.0, jnp.sqrt(F32(128 * rows * LANES)) / (jnp.sqrt(norm) + 1e-06))

    for q, (k, h) in enumerate(streams):
        at = pl.ds(*spans[k][h])
        clipped = clip * s["sum"][q][2][0]
        m_new = 0.5 * s["window"][0, at] + 0.5 * clipped
        v_new = 0.95 * s["window"][1, at] + 0.05 * clipped * clipped
        direction = m_new / (1.0 - 0.5**20) / (jnp.sqrt(v_new / (1.0 - 0.95**20)) + 1e-08)
        weights = s["master"][at]
        weights = weights - 0.05 * (direction + 0.1 * weights)
        master_out[at] = weights
        m_out[at] = m_new
        v_out[at] = v_new
        params[coords[0], coords[1], coords[2], core, at] = weights.astype(BF16)

    def spot(k, low, size, first, second_, third=None):
        at = [None] * 3
        one, two, three = ORDERS[k]
        at[one] = (coords[one] + first + 4) % 4
        at[two] = (coords[two] + second_ + 4) % 4
        at[three] = slice(None) if third is None else (coords[three] + third + 4) % 4
        return params.at[at[0], at[1], at[2], core, pl.ds(low, size)]

    def whole(k):
        return spans[k][0][0], spans[k][0][1] + spans[k][1][1]

    def share(k, first, second_):
        ref = spot(k, *whole(k), first, second_)
        launch(remote(ref, ref, s["sent"].at[8], s["shared"], partner))

    hops = {}

    def send(name, k, ref, dim, step):
        stage = {"third": 0, "second": 1, "second_far": 1, "first": 2, "first_far": 2}[name[0]]
        base = {"third": 0, "second": 1, "second_far": 3, "first": 4, "first_far": 12}[name[0]]
        rest = {"second": lambda i: i, "first": lambda line, i: 2 * line + i, "first_far": lambda line, i: line}
        i = base + rest.get(name[0], lambda i: 0)(*name[1:])
        hops[(k, *name)] = launch(remote(ref, ref, s["sent"].at[5 + stage], s["ag_in"].at[k, i], moved(dim, step)))

    around = ((0, 1), (1, -1))

    def forward(k, second_):
        for i, step in around:
            send(("first", second_ % 4, i), k, spot(k, *whole(k), 0, second_), ORDERS[k][0], step)

    def near(k, second_):
        for i, step in around:
            hops[k, "first", second_ % 4, i].wait_recv()
            send(("first_far", second_ % 4, i), k, spot(k, *spans[k][i], -step, second_), ORDERS[k][0], step)
            share(k, -step, second_)

    def far(k, second_):
        settled(spot(k, *whole(k), 2, second_), s["ag_in"].at[k, 12 + second_ % 4])
        share(k, 2, second_)

    for k in range(3):
        for i, step in enumerate((1, -1, 2)):
            send(("third", i), k, spot(k, *whole(k), 0, 0, 0), ORDERS[k][2], step)
    for k in range(3):
        settled(params.at[0, 0, pl.ds(0, 3), core, pl.ds(*whole(k))], s["ag_in"].at[k, 0])
        for i, step in around:
            send(("second", i), k, spot(k, *whole(k), 0, 0), ORDERS[k][1], step)
        forward(k, 0)
        share(k, 0, 0)
    for k in range(3):
        for i, step in around:
            hops[k, "second", i].wait_recv()
            send(("second_far", i), k, spot(k, *spans[k][i], 0, -step), ORDERS[k][1], step)
            forward(k, -step)
            share(k, 0, -step)
    for k in range(3):
        near(k, 0)
    for k in range(3):
        settled(spot(k, *whole(k), 0, 2), s["ag_in"].at[k, 3])
        forward(k, 2)
        share(k, 0, 2)
    for second_ in (1, -1, 2):
        for k in range(3):
            near(k, second_)
        for k in range(3):
            far(k, {1: 0, -1: 1, 2: -1}[second_])
    for k in range(3):
        far(k, 2)
    settled(params.at[:, :, :, other], s["shared"])
    lots = [params.at[pl.ds(0, 3), 0, 0, 0], params.at[pl.ds(0, 3), :, 0, 0], params.at[pl.ds(0, 3), :, :, 0]]
    everything = params.at[:, :, :, 0]
    for i, ref in enumerate([everything, *lots[::-1], s["norm_in"], *lots, everything]):
        settled(ref, s["sent"].at[i])
    for copy in moments_out:
        copy.wait_send()


def moments(s, rows, small, bounds, me, launch, remote, after, before):
    small[0].wait()
    loaded = s["old"].at[:, pl.ds(rows, 2 * rows)]
    pltpu.make_async_copy(loaded, loaded, s["small"].at[1]).wait()
    half = rows // 2
    begin = (me * rows + half) * LANES - bounds[me]
    begin = jnp.clip(begin, 0, rows * LANES)
    row, lane = begin // LANES, begin % LANES
    keep = lax.broadcasted_iota(jnp.int32, (CUT, LANES), 1) < LANES - lane
    blank = jnp.zeros((8, LANES), F32)
    for i in range(2):

        def clear(t, carry, i=i):
            s["old"][i, pl.ds(pl.multiple_of(8 * t, 8), 8)] = blank
            return carry

        lax.fori_loop(0, rows // 8, clear, 0)
        s["old"][i, 3 * rows : 3 * rows + 8] = blank

        def shifted(at, i=i):
            first = s["old"][i, pl.ds(row + at, CUT)]
            second = s["old"][i, pl.ds(row + at + 1, CUT)]
            return jnp.where(keep, pltpu.roll(first, LANES - lane, 1), pltpu.roll(second, LANES - lane, 1))

        def ends(t, carry, i=i, shifted=shifted):
            at = pl.multiple_of(CUT * t, CUT)
            for ref, base in ((s["head"], 0), (s["tail"], half + rows)):
                ref[i, pl.ds(at, CUT)] = shifted(base + at).astype(BF16)
            return carry

        lax.fori_loop(0, half // CUT, ends, 0)

        def middle(t, carry, i=i, shifted=shifted):
            at = pl.multiple_of(CUT * t, CUT)
            s["window"][i, pl.ds(at, CUT)] = shifted(half + at)
            return carry

        lax.fori_loop(0, rows // CUT, middle, 0)
    return [
        launch(remote(s["tail"], s["from_before"], s["mom_out"].at[0], s["mom_in"].at[0], after)),
        launch(remote(s["head"], s["from_after"], s["mom_out"].at[1], s["mom_in"].at[1], before)),
    ]


def second(s, rs, launch, loop, coords, q, k, h, sign, phase, count):
    place = coords[ORDERS[k][phase]]
    pieces = ((FAR, 2), (DIRECT, -sign[h]), (RELAY, sign[h]))
    for kind, step in pieces[: phase + 1]:
        at = ((place + step + 4) % 4) * count

        def body(t, kind=kind, at=at):
            s["out"][q][phase][kind, t] = s["sum"][q][phase - 1][at + t].astype(BF16)

        loop(count, body)
        launch(rs[q, phase, kind])


def relay(s, rs, launch, loop, coords, q, k, h, sign, phase, count):
    place = coords[ORDERS[k][phase]]
    rs[q, phase, FAR].wait_recv()
    at = ((place + sign[h] + 4) % 4) * count

    def body(t):
        value = s["sum"][q][phase - 1][at + t] + s["in"][q][phase][FAR, t].astype(F32)
        s["out"][q][phase][RELAY, t] = value.astype(BF16)

    loop(count, body)
    launch(rs[q, phase, RELAY])


def finish(s, rs, loop, coords, q, k, phase, count):
    place = coords[ORDERS[k][phase]]
    kinds = (FAR, DIRECT, RELAY) if phase == 2 else (DIRECT, RELAY)
    arrived = s["in"][q][phase].at[pl.ds(kinds[0], len(kinds))]
    pltpu.make_async_copy(arrived, arrived, s["rs_in"].at[q, phase, 1]).wait()
    at = place * count

    def body(t):
        value = s["sum"][q][phase - 1][at + t]
        for kind in kinds:
            value += s["in"][q][phase][kind, t].astype(F32)
        s["sum"][q][phase][t] = value

    loop(count, body)


def step(g, master, m_old, v_old, bounds):
    rows = master.shape[0]
    spans = plan(rows)
    sizes = [a[1] + b[1] for a, b in spans]
    dma = pltpu.SemaphoreType.DMA
    halves = [span for colour in spans for span in colour]
    scratch = {
        "theirs": [pltpu.VMEM((4, 4, 4, n, LANES), F32) for n in sizes],
        "ours": [pltpu.VMEM((4, 4, 4, n, LANES), F32) for n in sizes],
        "give": [pltpu.VMEM((4, 4, 4, n, LANES), BF16) for n in sizes],
        "take": [pltpu.VMEM((4, 4, 4, n, LANES), BF16) for n in sizes],
        "out": [[pltpu.VMEM((3, m, n, LANES), BF16) for m in (16, 4, 1)] for _, n in halves],
        "in": [[pltpu.VMEM((3, m, n, LANES), BF16) for m in (16, 4, 1)] for _, n in halves],
        "sum": [[pltpu.VMEM((m, n, LANES), F32) for m in (16, 4, 1)] for _, n in halves],
        "master": pltpu.VMEM((rows, LANES), F32),
        "old": pltpu.VMEM((2, 3 * rows + 8, LANES), F32),
        "window": pltpu.VMEM((2, rows, LANES), F32),
        "tail": pltpu.VMEM((2, rows // 2, LANES), BF16),
        "head": pltpu.VMEM((2, rows // 2, LANES), BF16),
        "from_before": pltpu.VMEM((2, rows // 2, LANES), BF16),
        "from_after": pltpu.VMEM((2, rows // 2, LANES), BF16),
        "norm": pltpu.VMEM((3, 1, LANES), F32),
        "norm_in": pltpu.VMEM((22, 1, LANES), F32),
        "load": dma((3, 4, 2)),
        "small": dma((2,)),
        "swap_in": dma((3, 4)),
        "sent": dma((9,)),
        "rs_in": dma((6, 3, 2)),
        "mom_out": dma((2,)),
        "mom_in": dma((2,)),
        "norm_got": dma((2,)),
        "ag_in": dma((3, 16)),
        "shared": dma(()),
    }
    leaves, tree = jax.tree.flatten(scratch)

    def body(*refs):
        kernel(
            spans,
            rows,
            {"in": refs[:5], "out": refs[5:9], "scratch": jax.tree.unflatten(tree, refs[9:])},
        )

    whole = pl.BlockSpec(memory_space=pl.ANY)
    vmem = pl.BlockSpec(memory_space=pltpu.VMEM)
    return pl.pallas_call(
        body,
        name="adam_step",
        out_shape=(
            pltpu.VMEM((rows, LANES), F32),
            pltpu.VMEM((rows, LANES), F32),
            pltpu.VMEM((rows, LANES), F32),
            pltpu.VMEM((4, 4, 4, 2, rows, LANES), BF16),
        ),
        in_specs=[whole] * 4 + [pl.BlockSpec(memory_space=pltpu.SMEM)],
        out_specs=[vmem] * 4,
        scratch_shapes=leaves,
        compiler_params=pltpu.CompilerParams(collective_id=0, has_side_effects=True, vmem_limit_bytes=48 * 2**20),
    )(g, master, m_old, v_old, bounds)


def flush_body(*refs):
    count = len(refs) // 2
    copies = [pltpu.make_async_copy(refs[i], refs[count + i], refs[-1].at[i]) for i in range(count)]
    for copy in copies:
        copy.start()
    for copy in copies:
        copy.wait()


def flush(arrays):
    return pl.pallas_call(
        flush_body,
        name="flush",
        out_shape=tuple(jax.ShapeDtypeStruct(a.shape, a.dtype) for a in arrays),
        in_specs=[pl.BlockSpec(memory_space=pltpu.VMEM)] * len(arrays),
        out_specs=[pl.BlockSpec(memory_space=pl.ANY)] * len(arrays),
        scratch_shapes=[pltpu.SemaphoreType.DMA((len(arrays),))],
        compiler_params=pltpu.CompilerParams(vmem_limit_bytes=2**20),
    )(*arrays)


def local(grads, master, m_old, v_old, old_bounds):
    width = master.shape[0]
    rows = width // LANES
    results = step(
        grads.reshape(4, 4, 4, 2, rows, LANES),
        master.reshape(rows, LANES),
        m_old.reshape(2 * rows, LANES),
        v_old.reshape(2 * rows, LANES),
        old_bounds,
    )
    return tuple(a.reshape(-1) for a in flush(results))


def solution(mesh):
    finer = Mesh(mesh.devices.reshape(4, 4, 4, 2), DP)
    placed = (P(DP, None), P(DP), P(DP, None), P(DP, None), P())
    return jax.shard_map(local, mesh=finer, in_specs=placed, out_specs=(P(DP), P(DP), P(DP), P()), check_vma=False)
```

time: 110 us -> 79 us (0.72)
  local copies, waits for them, and re-layouts: 15 us -> 0 us
  Pallas kernels: 91.6 us -> 78.3 us
  other arithmetic: 1.56 us -> 0 us
    pallas_call x1 -> x2, Pallas kernels: 91.6 us -> 78.3 us  [the longest x1 74.7 us: step(): pl.pallas_call(body, name='adam_step', out_shape=(pltpu.VMEM((rows, LANES...]
    unnamed x7 -> x0, local copies, waits for them, and re-layouts: 13.1 us -> none
    concatenate x1 -> x0, other arithmetic: 1.56 us -> none  [local(): packed = jnp.concatenate([m_old, v_old])]
    dynamic_slice x1 -> x0, local copies, waits for them, and re-layouts: 1.27 us -> none  [local(): begin = device * width - old_bounds[device]]
where the time goes in v2:
time: 79 us; the launch traced here: 78.9 us
  Pallas kernels  78.3 us (99%)
    pallas_call x1, Pallas kernels, step(): pl.pallas_call(body, name='adam_step', out_shape=(pltpu.VMEM((rows, LANES...  74.7 us
    pallas_call x1, Pallas kernels, flush(): pl.pallas_call(flush_body, name='flush', out_shape=tuple((jax.ShapeDtypeS...  3.56 us

profile of v2, /device:TPU:1, one launch (start us, length us, event | category | flops | bytes accessed | tf_op | source)
XLA Modules:
  0.0 78.9 jit_solution(6707152808827508527)
XLA Ops:
  0.6 74.7 %adam_step.1 = (f32[256,128]{1,0:T(8,128)S(1)}, f32[256,128]{1,0:T(8,128)S(1)}, f32[256,128]{1,0:T(8,128)S(1)}, bf16[4,4,4,2,256,128]{5,4,3,2,1,0:T(8,128)(2,1)S(1)}) custom-call(f32[4,4,4,2,256,128]{5,4,3,2,1,0:T(8,128)} %bitcast.8, f32[256,128]{1,0:T(8,128)} %bitcast.11, f32[512,128]{1,0:T(8,128)} %bitcast.9, f32[512,128]{1,0:T(8,128)} %bitcast.10, s32[129]{0:T(256)} %refs_4_.1), custom_call_target="tpu_custom_call" | custom-call | tf_op jit(solution)/shard_map/adam_step/pallas_call | solution.py:472
  75.4 3.6 %flush.1 = (f32[256,128]{1,0:T(8,128)}, f32[256,128]{1,0:T(8,128)}, f32[256,128]{1,0:T(8,128)}, bf16[4,4,4,2,256,128]{5,4,3,2,1,0:T(8,128)(2,1)}) custom-call(f32[256,128]{1,0:T(8,128)S(1)} %get-tuple-element.12.refs_0_, f32[256,128]{1,0:T(8,128)S(1)} %get-tuple-element.13.refs_1_, f32[256,128]{1,0:T(8,128)S(1)} %get-tuple-element.14.refs_2_, ...), custom_call_target="tpu_custom_call" | custom-call | tf_op jit(solution)/shard_map/flush/pallas_call | solution.py:498

commit v3 on v2

--- a/solution.py
+++ b/solution.py
@@ -107,10 +107,11 @@
         lax.fori_loop(0, 16, body, 0)
         launch(swaps[k, slot])
 
-    def joined(k, slot, h, t):
-        u, v = (t // 4, t % 4) if ORDERS[k][1] < ORDERS[k][2] else (t % 4, t // 4)
-        low = spans[k][h][0] - spans[k][0][0]
-        at = pl.ds(low, spans[k][h][1])
+    def joined(k, slot, h, second, third):
+        _, two, three = ORDERS[k]
+        i2, i3 = (coords[two] + second) % 4, (coords[three] + third) % 4
+        u, v = (i2, i3) if two < three else (i3, i2)
+        at = pl.ds(spans[k][h][0] - spans[k][0][0], spans[k][h][1])
         return s["ours"][k][slot, u, v, at] + s["take"][k][slot, u, v, at].astype(F32)
 
     def arrive(k, slot):
@@ -120,21 +121,16 @@
     streams = [(k, h) for k in range(3) for h in range(2)]
     sign = {0: 1, 1: -1}
 
-    def steps_of(h, phase):
-        return ((FAR, 2 if phase == 2 else sign[h]), (DIRECT, -sign[h]), (RELAY, sign[h]))
-
-    rs = {}
-    for q, (k, h) in enumerate(streams):
-        for phase in range(3):
-            dim = ORDERS[k][phase]
-            for kind, step in steps_of(h, phase):
-                rs[q, phase, kind] = remote(
-                    s["out"][q][phase].at[kind],
-                    s["in"][q][phase].at[kind],
-                    s["sent"].at[1 + phase],
-                    s["rs_in"].at[q, phase, 0 if kind == FAR and phase < 2 else 1],
-                    moved(dim, step),
-                )
+    def hop(q, phase, kind, line=None):
+        k, h = streams[q]
+        step = {FAR: 2 if phase == 2 else sign[h], DIRECT: -sign[h], RELAY: sign[h]}[kind]
+        src, dst = s["out"][q][phase].at[kind], s["in"][q][phase].at[kind]
+        group = 0 if kind == FAR and phase < 2 else 1
+        got = s["rs_in"].at[q, max(phase - 1, 0), group]
+        if line is not None:
+            src, dst = src.at[pl.ds(4 * line, 4)], dst.at[pl.ds(4 * line, 4)]
+            got = s["rs_line"].at[q, group, line]
+        return remote(src, dst, s["sent"].at[1 + phase], got, moved(ORDERS[k][phase], step))
 
     def loop(count, body):
         def step(t, carry):
@@ -143,66 +139,113 @@
 
         lax.fori_loop(0, count, step, 0)
 
+    def first(q, kind, place):
+        k, h = streams[q]
+        line = order[h][place]
+        slot = {FAR: 2, DIRECT: -sign[h] % 4, RELAY: sign[h] % 4}[kind]
+        if kind == RELAY:
+            hop(q, 0, FAR, line).wait_recv()
+
+        def body(t):
+            value = joined(k, slot, h, line, t)
+            if kind == RELAY:
+                value += s["in"][q][0][FAR, 4 * line + t].astype(F32)
+            s["out"][q][0][kind, 4 * line + t] = value.astype(BF16)
+
+        loop(4, body)
+        launch(hop(q, 0, kind, line))
+
+    def finished(q, place):
+        k, h = streams[q]
+        line = order[h][place]
+        settled(s["in"][q][0].at[pl.ds(DIRECT, 2), pl.ds(4 * line, 4)], s["rs_line"].at[q, 1, line])
+
+        def body(t):
+            got = s["in"][q][0]
+            value = joined(k, 0, h, line, t)
+            value += got[DIRECT, 4 * line + t].astype(F32) + got[RELAY, 4 * line + t].astype(F32)
+            if place < 2:
+                s["out"][q][1][(FAR, DIRECT)[place], t] = value.astype(BF16)
+            else:
+                s["sum"][q][0][place - 2, t] = value
+
+        loop(4, body)
+        if place < 2:
+            launch(hop(q, 1, (FAR, DIRECT)[place]))
+
+    def relayed(q):
+        hop(q, 1, FAR).wait_recv()
+
+        def body(t):
+            value = s["sum"][q][0][0, t] + s["in"][q][1][FAR, t].astype(F32)
+            s["out"][q][1][RELAY, t] = value.astype(BF16)
+
+        loop(4, body)
+        launch(hop(q, 1, RELAY))
+
+    def second(q):
+        _, h = streams[q]
+        settled(s["in"][q][1].at[pl.ds(DIRECT, 2)], s["rs_in"].at[q, 0, 1])
+        for kind, third in ((FAR, 2), (DIRECT, -sign[h] % 4), (RELAY, sign[h] % 4), (None, 0)):
+            got = s["in"][q][1]
+            value = s["sum"][q][0][1, third] + got[DIRECT, third].astype(F32) + got[RELAY, third].astype(F32)
+            if kind is None:
+                s["sum"][q][1][...] = value
+            else:
+                s["out"][q][2][kind, 0] = value.astype(BF16)
+                launch(hop(q, 2, kind))
+
+    def third(q):
+        got = s["in"][q][2]
+        settled(got, s["rs_in"].at[q, 1, 1])
+        value = s["sum"][q][1][...]
+        for kind in (FAR, DIRECT, RELAY):
+            value += got[kind, 0].astype(F32)
+        s["sum"][q][2][...] = value
+        return value * value
+
+    order = [(2, -sign[h] % 4, sign[h] % 4, 0) for h in range(2)]
     for k in range(3):
         narrow(k, 2)
     for k in range(3):
         narrow(k, 3)
         arrive(k, 2)
         for h in range(2):
-            q = 2 * k + h
-
-            def body(t, k=k, h=h, q=q):
-                s["out"][q][0][FAR, t] = joined(k, 2, h, t).astype(BF16)
-
-            loop(16, body)
-            launch(rs[q, 0, FAR])
+            for place in range(4):
+                first(2 * k + h, FAR, place)
     for k in range(3):
         narrow(k, 1)
-    for h, slot in ((0, 3), (1, 1)):
+    for h in range(2):
         for k in range(3):
-            q = 2 * k + h
-            arrive(k, slot)
-
-            def body(t, k=k, h=h, q=q, slot=slot):
-                s["out"][q][0][DIRECT, t] = joined(k, slot, h, t).astype(BF16)
-
-            loop(16, body)
-            launch(rs[q, 0, DIRECT])
+            arrive(k, -sign[h] % 4)
+            for place in range(2):
+                first(2 * k + h, DIRECT, place)
     for k in range(3):
         narrow(k, 0)
-    for q, (k, h) in enumerate(streams):
-        rs[q, 0, FAR].wait_recv()
-
-        def body(t, k=k, h=h, q=q):
-            value = joined(k, sign[h] % 4, h, t) + s["in"][q][0][FAR, t].astype(F32)
-            s["out"][q][0][RELAY, t] = value.astype(BF16)
-
-        loop(16, body)
-        launch(rs[q, 0, RELAY])
-
+    for kind, place in ((RELAY, 0), (DIRECT, 2), (RELAY, 1), (DIRECT, 3)):
+        for q in range(6):
+            first(q, kind, place)
     moments_out = moments(s, rows, small, bounds, me, launch, remote, after, before)
+    for q in range(6):
+        first(q, RELAY, 2)
     for k in range(3):
         arrive(k, 0)
-    for q, (k, h) in enumerate(streams):
-        settled(s["in"][q][0].at[pl.ds(DIRECT, 2)], s["rs_in"].at[q, 0, 1])
-
-        def body(t, k=k, h=h, q=q):
-            got = s["in"][q][0]
-            s["sum"][q][0][t] = joined(k, 0, h, t) + got[DIRECT, t].astype(F32) + got[RELAY, t].astype(F32)
-
-        loop(16, body)
-        if True:
-            second(s, rs, launch, loop, coords, q, k, h, sign, 1, 4)
-    for q, (k, h) in enumerate(streams):
-        relay(s, rs, launch, loop, coords, q, k, h, sign, 1, 4)
-    for q, (k, h) in enumerate(streams):
-        finish(s, rs, loop, coords, q, k, 1, 4)
-        second(s, rs, launch, loop, coords, q, k, h, sign, 2, 1)
+    for q in range(6):
+        finished(q, 0)
+    for q in range(6):
+        first(q, RELAY, 3)
+    for q in range(6):
+        finished(q, 1)
+    for q in range(6):
+        finished(q, 2)
+        relayed(q)
+    for q in range(6):
+        finished(q, 3)
+    for q in range(6):
+        second(q)
     total = jnp.zeros((8, LANES), F32)
     for q, (k, h) in enumerate(streams):
-        finish(s, rs, loop, coords, q, k, 2, 1)
-        value = s["sum"][q][2][0]
-        square = value * value
+        square = third(q)
         for i in range(spans[k][h][1] // 8):
             total += square[8 * i : 8 * i + 8]
 
@@ -250,7 +293,7 @@
 
     for q, (k, h) in enumerate(streams):
         at = pl.ds(*spans[k][h])
-        clipped = clip * s["sum"][q][2][0]
+        clipped = clip * s["sum"][q][2][...]
         m_new = 0.5 * s["window"][0, at] + 0.5 * clipped
         v_new = 0.95 * s["window"][1, at] + 0.05 * clipped * clipped
         direction = m_new / (1.0 - 0.5**20) / (jnp.sqrt(v_new / (1.0 - 0.95**20)) + 1e-08)
@@ -308,12 +351,15 @@
         settled(params.at[0, 0, pl.ds(0, 3), core, pl.ds(*whole(k))], s["ag_in"].at[k, 0])
         for i, step in around:
             send(("second", i), k, spot(k, *whole(k), 0, 0), ORDERS[k][1], step)
+    for k in range(3):
         forward(k, 0)
         share(k, 0, 0)
     for k in range(3):
         for i, step in around:
             hops[k, "second", i].wait_recv()
             send(("second_far", i), k, spot(k, *spans[k][i], 0, -step), ORDERS[k][1], step)
+    for k in range(3):
+        for i, step in around:
             forward(k, -step)
             share(k, 0, -step)
     for k in range(3):
@@ -380,48 +426,6 @@
         launch(remote(s["tail"], s["from_before"], s["mom_out"].at[0], s["mom_in"].at[0], after)),
         launch(remote(s["head"], s["from_after"], s["mom_out"].at[1], s["mom_in"].at[1], before)),
     ]
-
-
-def second(s, rs, launch, loop, coords, q, k, h, sign, phase, count):
-    place = coords[ORDERS[k][phase]]
-    pieces = ((FAR, 2), (DIRECT, -sign[h]), (RELAY, sign[h]))
-    for kind, step in pieces[: phase + 1]:
-        at = ((place + step + 4) % 4) * count
-
-        def body(t, kind=kind, at=at):
-            s["out"][q][phase][kind, t] = s["sum"][q][phase - 1][at + t].astype(BF16)
-
-        loop(count, body)
-        launch(rs[q, phase, kind])
-
-
-def relay(s, rs, launch, loop, coords, q, k, h, sign, phase, count):
-    place = coords[ORDERS[k][phase]]
-    rs[q, phase, FAR].wait_recv()
-    at = ((place + sign[h] + 4) % 4) * count
-
-    def body(t):
-        value = s["sum"][q][phase - 1][at + t] + s["in"][q][phase][FAR, t].astype(F32)
-        s["out"][q][phase][RELAY, t] = value.astype(BF16)
-
-    loop(count, body)
-    launch(rs[q, phase, RELAY])
-
-
-def finish(s, rs, loop, coords, q, k, phase, count):
-    place = coords[ORDERS[k][phase]]
-    kinds = (FAR, DIRECT, RELAY) if phase == 2 else (DIRECT, RELAY)
-    arrived = s["in"][q][phase].at[pl.ds(kinds[0], len(kinds))]
-    pltpu.make_async_copy(arrived, arrived, s["rs_in"].at[q, phase, 1]).wait()
-    at = place * count
-
-    def body(t):
-        value = s["sum"][q][phase - 1][at + t]
-        for kind in kinds:
-            value += s["in"][q][phase][kind, t].astype(F32)
-        s["sum"][q][phase][t] = value
-
-    loop(count, body)
 
 
 def step(g, master, m_old, v_old, bounds):
@@ -437,7 +441,9 @@
         "take": [pltpu.VMEM((4, 4, 4, n, LANES), BF16) for n in sizes],
         "out": [[pltpu.VMEM((3, m, n, LANES), BF16) for m in (16, 4, 1)] for _, n in halves],
         "in": [[pltpu.VMEM((3, m, n, LANES), BF16) for m in (16, 4, 1)] for _, n in halves],
-        "sum": [[pltpu.VMEM((m, n, LANES), F32) for m in (16, 4, 1)] for _, n in halves],
+        "sum": [
+            [pltpu.VMEM((2, 4, n, LANES), F32), pltpu.VMEM((n, LANES), F32), pltpu.VMEM((n, LANES), F32)] for _, n in halves
+        ],
         "master": pltpu.VMEM((rows, LANES), F32),
         "old": pltpu.VMEM((2, 3 * rows + 8, LANES), F32),
         "window": pltpu.VMEM((2, rows, LANES), F32),
@@ -451,7 +457,8 @@
         "small": dma((2,)),
         "swap_in": dma((3, 4)),
         "sent": dma((9,)),
-        "rs_in": dma((6, 3, 2)),
+        "rs_line": dma((6, 2, 4)),
+        "rs_in": dma((6, 2, 2)),
         "mom_out": dma((2,)),
         "mom_in": dma((2,)),
         "norm_got": dma((2,)),

time: 79 us -> 73.2 us (0.927)
  Pallas kernels: 78.3 us -> 72.4 us
    pallas_call x1, Pallas kernels: 74.7 us -> 68.9 us  [step(): pl.pallas_call(body, name='adam_step', out_shape=(pltpu.VMEM((rows, LANES...]
where the time goes in v3:
time: 73.2 us; the launch traced here: 73.1 us
  Pallas kernels  72.4 us (99%)
    pallas_call x1, Pallas kernels, step(): pl.pallas_call(body, name='adam_step', out_shape=(pltpu.VMEM((rows, LANES...  68.9 us
    pallas_call x1, Pallas kernels, flush(): pl.pallas_call(flush_body, name='flush', out_shape=tuple((jax.ShapeDtypeS...  3.56 us

profile of v3, /device:TPU:1, one launch (start us, length us, event | category | flops | bytes accessed | tf_op | source)
XLA Modules:
  0.0 73.1 jit_solution(6941235423183002676)
XLA Ops:
  0.6 68.9 %adam_step.1 = (f32[256,128]{1,0:T(8,128)S(1)}, f32[256,128]{1,0:T(8,128)S(1)}, f32[256,128]{1,0:T(8,128)S(1)}, bf16[4,4,4,2,256,128]{5,4,3,2,1,0:T(8,128)(2,1)S(1)}) custom-call(f32[4,4,4,2,256,128]{5,4,3,2,1,0:T(8,128)} %bitcast.8, f32[256,128]{1,0:T(8,128)} %bitcast.11, f32[512,128]{1,0:T(8,128)} %bitcast.9, f32[512,128]{1,0:T(8,128)} %bitcast.10, s32[129]{0:T(256)} %refs_4_.1), custom_call_target="tpu_custom_call" | custom-call | tf_op jit(solution)/shard_map/adam_step/pallas_call | solution.py:479
  69.5 3.6 %flush.1 = (f32[256,128]{1,0:T(8,128)}, f32[256,128]{1,0:T(8,128)}, f32[256,128]{1,0:T(8,128)}, bf16[4,4,4,2,256,128]{5,4,3,2,1,0:T(8,128)(2,1)}) custom-call(f32[256,128]{1,0:T(8,128)S(1)} %get-tuple-element.12.refs_0_, f32[256,128]{1,0:T(8,128)S(1)} %get-tuple-element.13.refs_1_, f32[256,128]{1,0:T(8,128)S(1)} %get-tuple-element.14.refs_2_, ...), custom_call_target="tpu_custom_call" | custom-call | tf_op jit(solution)/shard_map/flush/pallas_call | solution.py:505
